TPU v7x, 32 devices: a 4x4x1 block of a 4x4x8 slice. The times are simulated.
32 devices in a mesh: batch: 1 (over z), col: 4 (over y), row: 8 (over x, core).
Axes of the slice: x: 4, y: 4, z: 1, core: 2. Of those that a mesh axis runs over, the one named last changes fastest.
The devices are a block of a 4x4x8 slice.
Arguments:
- lower_cyc: float32 [2048, 2048], P(('batch', 'row'), 'col')
Outputs:
- output: float32 [2048, 2048], P(('batch', 'row'), 'col')
All inputs are finite; a program needn't handle non-finite values.
Results may differ from a plain program's by a relative error of at most 0.001.
Values sent between devices are 32-bit elements.
A program may use at most 768 MiB of HBM per device.

v0:
```python
import jax
import jax.numpy as jnp
from jax import lax
from jax.sharding import PartitionSpec as P

DEPTH = 3
BLK = 8


def highest_matmul(left, right):
    return jnp.einsum("sik,skj->sij", left, right, precision=lax.Precision.HIGHEST, preferred_element_type=jnp.float32)


def natural_inner_cols(gathered):
    num_sub, row_len, grid_len, col_len = gathered.shape
    split_view = gathered.reshape(num_sub, row_len, grid_len, col_len // BLK, BLK)
    return split_view.transpose(0, 1, 3, 2, 4).reshape(num_sub, row_len, grid_len * col_len)


def natural_inner_rows(gathered):
    num_sub, grid_len, row_len, col_len = gathered.shape
    split_view = gathered.reshape(num_sub, grid_len, row_len // BLK, BLK, col_len)
    return split_view.transpose(0, 2, 1, 3, 4).reshape(num_sub, grid_len * row_len, col_len)


def cyclic_product(left, right):
    left_panel = natural_inner_cols(lax.all_gather(left, "col", axis=2))
    right_panel = natural_inner_rows(lax.all_gather(right, "row", axis=1))
    return highest_matmul(left_panel, right_panel)


def leaf_inverses(local_l, grid_rows, grid_cols):
    row_idx = lax.axis_index("row")
    col_idx = lax.axis_index("col")
    leaves = 2 ** DEPTH
    row_len = local_l.shape[0] // leaves
    col_len = local_l.shape[1] // leaves
    blocks4 = local_l.reshape(leaves, row_len, leaves, col_len)
    diag_blocks = jnp.stack([blocks4[leaf_idx, :, leaf_idx, :] for leaf_idx in range(leaves)])
    gathered = lax.all_gather(lax.all_gather(diag_blocks, "row", axis=1), "col", axis=3)
    leaf_size = grid_rows * row_len
    split_view = gathered.reshape(leaves, grid_rows, row_len // BLK, BLK, grid_cols, col_len // BLK, BLK)
    natural = split_view.transpose(0, 2, 1, 3, 5, 4, 6).reshape(leaves, leaf_size, leaf_size)
    piece_len = col_len // grid_rows
    local_cols = row_idx * piece_len + jnp.arange(piece_len)
    target_cols = (local_cols // BLK) * (grid_cols * BLK) + col_idx * BLK + local_cols % BLK
    identity_cols = (jnp.arange(leaf_size)[:, None] == target_cols[None, :]).astype(jnp.float32)
    rhs_batch = jnp.broadcast_to(identity_cols, (leaves, leaf_size, piece_len))
    solved = lax.linalg.triangular_solve(natural, rhs_batch, left_side=True, lower=True)
    parted = solved.reshape(leaves, row_len // BLK, grid_rows, BLK, piece_len)
    owned_rows = lax.all_to_all(parted, "row", 2, 4, tiled=True)
    return owned_rows.reshape(leaves, row_len, col_len)


def solution(mesh):
    grid_rows = mesh.shape["row"]
    grid_cols = mesh.shape["col"]
    block_spec = P(("batch", "row"), "col")

    def device_body(local_l):
        inverse = leaf_inverses(local_l, grid_rows, grid_cols)
        for level_idx in reversed(range(DEPTH)):
            num_sub = 2 ** level_idx
            half_rows = inverse.shape[1]
            half_cols = inverse.shape[2]
            paired_inv = inverse.reshape(num_sub, 2, half_rows, half_cols)
            inv_upper = paired_inv[:, 0]
            inv_lower = paired_inv[:, 1]
            blocks6 = local_l.reshape(num_sub, 2, half_rows, num_sub, 2, half_cols)
            coupling = jnp.stack([blocks6[sub_idx, 1, :, sub_idx, 0, :] for sub_idx in range(num_sub)])
            temp_prod = cyclic_product(coupling, inv_upper)
            off_diag = -cyclic_product(inv_lower, temp_prod)
            upper_rows = jnp.concatenate([inv_upper, jnp.zeros_like(inv_upper)], axis=2)
            lower_rows = jnp.concatenate([off_diag, inv_lower], axis=2)
            inverse = jnp.concatenate([upper_rows, lower_rows], axis=1)
        return inverse.reshape(local_l.shape)

    return jax.shard_map(device_body, mesh=mesh, in_specs=(block_spec,), out_specs=block_spec, check_vma=False)
```

profile of v0, /device:TPU:97, one launch (start us, length us, event | category | flops | bytes accessed | tf_op | source)
XLA Modules:
  0.0 584.9 jit_solution(15408810518385005685)
XLA Ops:
  8.0 21.4 %all-gather = f32[8,256,64]{2,1,0:T(8,128)S(1)} all-gather(f32[8,32,64]{2,1,0:T(8,128)S(1)} %constant_dynamic-update-slice_fusion), channel_id=2, replica_groups=mesh['batch'=1,'col'=4,'row'=8] {'row'}, dimensions={1}, use_global_device_ids=true | all-gather | bytes 589824 | tf_op jit(solution)/shard_map/all_gather | solution.py:40
  29.5 2.9 copy.212
  33.7 12.2 %all-gather.3 = f32[4,32,256]{1,0,2:T(4,128)S(1)} all-gather(f32[4,32,64]{1,0,2:T(4,128)S(1)} %copy.229), channel_id=5, replica_groups=mesh['batch'=1,'col'=4,'row'=8] {'col'}, dimensions={2}, use_global_device_ids=true | all-gather | bytes 163840 | tf_op jit(solution)/shard_map/all_gather | solution.py:27
  46.2 73.5 %all-gather.17.cloned.1.call-done = f32[8,8,32,256]{2,1,0,3:T(8,128)} async-done(((f32[8,8,32,64]{2,1,0,3:T(8,128)}), f32[8,8,32,256]{2,1,0,3:T(8,128)}) %all-gather.17.cloned.1.call-update) | async-done | bytes 2097168 | tf_op jit(solution)/shard_map/all_gather | solution.py:40
  119.8 6.3 %copy.213 = f32[8,8,32,256]{3,2,1,0:T(8,128)S(1)} copy(f32[8,8,32,256]{2,1,0,3:T(8,128)} %all-gather.17.cloned.1.call-done) | data formatting | bytes 4194304 | tf_op jit(solution)/shard_map/all_gather | solution.py:40
  126.0 21.1 %reshape.153 = f32[8,8,4,8,4,8,8]{6,5,4,3,2,1,0:T(8,128)} reshape(f32[8,8,32,256]{3,2,1,0:T(8,128)S(1)} %copy.213) | data formatting | bytes 4194304 | tf_op jit(solution)/shard_map/reshape | solution.py:42
  147.1 25.0 %copy.266 = f32[8,4,8,8,8,4,8]{6,5,4,3,2,1,0:T(4,128)} copy(f32[8,4,8,8,8,4,8]{6,4,5,3,1,2,0:T(8,128)} %bitcast.169) | data formatting | bytes 4194304 | tf_op jit(solution)/shard_map/reshape | solution.py:43
  172.1 41.2 %reshape.228 = f32[8,256,256]{2,1,0:T(8,128)} reshape(f32[8,4,8,8,8,4,8]{6,5,4,3,2,1,0:T(4,128)} %copy.266) | data formatting | bytes 4194304 | tf_op jit(solution)/shard_map/reshape | solution.py:43
  215.2 5.9 %while.1 = (s32[]{:T(128)}, f32[8,256,256]{2,1,0:T(8,128)S(1)}, s32[2,2]{1,0:T(2,128)S(1)}, f32[2,8,128,128]{3,2,0,1:T(8,128)}, s32[]{:T(128)}) while((s32[]{:T(128)}, f32[8,256,256]{2,1,0:T(8,128)S(1)}, s32[2,2]{1,0:T(2,128)S(1)}, f32[2,8,128,128]{3,2,0,1:T(8,128)}, s32[]{:T(128)}) %tuple.40), condition=%wide.while_cond, body=%wide.while_body.sunk | while | flops 2 | bytes 1050209 | solution.py:49
  215.9 2.3 bitcast_dynamic-update-slice_fusion.2
  221.1 158.6 %custom-call.3 = f32[8,2,128,128]{2,3,1,0:T(8,128)} custom-call(f32[8,2,128,128]{3,2,1,0:T(8,128)} %bitcast.211), custom_call_target="InvertDiagBlocksLowerTriangular" | custom-call | tf_op jit(solution)/shard_map/triangular_solve | solution.py:49
  386.2 4.5 all-to-all-start
  390.7 9.9 %all-gather.6 = f32[2,64,512]{2,1,0:T(8,128)S(1)} all-gather(f32[2,64,128]{2,1,0:T(8,128)S(1)} %pad_maximum_fusion.2), channel_id=8, replica_groups=mesh['batch'=1,'col'=4,'row'=8] {'col'}, dimensions={2}, use_global_device_ids=true | all-gather | bytes 327680 | tf_op jit(solution)/shard_map/all_gather | solution.py:27
  404.7 20.2 %all_gather.70 = f32[4,8,32,64]{3,2,0,1:T(8,128)S(1)} all-gather(f32[4,1,32,64]{3,2,0,1:T(8,128)S(1)} %get-tuple-element.45), channel_id=1, replica_groups=mesh['batch'=1,'col'=4,'row'=8] {'row'}, dimensions={1}, use_global_device_ids=true | all-gather | bytes 294912 | tf_op jit(solution)/shard_map/all_gather | solution.py:28
  426.0 22.5 %all-gather.4 = f32[4,256,64]{2,1,0:T(8,128)S(1)} all-gather(f32[4,32,64]{2,1,0:T(8,128)S(1)} %fusion.14), channel_id=6, replica_groups=mesh['batch'=1,'col'=4,'row'=8] {'row'}, dimensions={1}, use_global_device_ids=true | all-gather | bytes 294912 | tf_op jit(solution)/shard_map/all_gather | solution.py:28
  448.7 10.2 %all-gather.2 = f32[4,1,32,256]{2,0,1,3:T(4,128)S(1)} all-gather(f32[4,1,32,64]{2,0,1,3:T(4,128)S(1)} %copy.223), channel_id=4, replica_groups=mesh['batch'=1,'col'=4,'row'=8] {'col'}, dimensions={3}, use_global_device_ids=true | all-gather | bytes 163840 | tf_op jit(solution)/shard_map/all_gather | solution.py:27
  460.2 25.4 %all_gather.76 = f32[2,8,64,128]{3,2,0,1:T(8,128)S(1)} all-gather(f32[2,1,64,128]{3,2,0,1:T(8,128)S(1)} %get-tuple-element.41), channel_id=1, replica_groups=mesh['batch'=1,'col'=4,'row'=8] {'row'}, dimensions={1}, use_global_device_ids=true | all-gather | bytes 589824 | tf_op jit(solution)/shard_map/all_gather | solution.py:28
  486.7 22.6 %all-gather.7 = f32[2,512,128]{2,1,0:T(8,128)S(1)} all-gather(f32[2,64,128]{2,1,0:T(8,128)S(1)} %fusion.15), channel_id=9, replica_groups=mesh['batch'=1,'col'=4,'row'=8] {'row'}, dimensions={1}, use_global_device_ids=true | all-gather | bytes 589824 | tf_op jit(solution)/shard_map/all_gather | solution.py:28
  509.3 9.4 %all-gather.5 = f32[2,1,64,512]{3,2,0,1:T(8,128)S(1)} all-gather(f32[2,1,64,128]{3,2,0,1:T(8,128)S(1)} %get-tuple-element.44), channel_id=7, replica_groups=mesh['batch'=1,'col'=4,'row'=8] {'col'}, dimensions={3}, use_global_device_ids=true | all-gather | bytes 327680 | tf_op jit(solution)/shard_map/all_gather | solution.py:27
  521.6 10.3 %all-gather.9 = f32[1,1,128,4,1,256]{5,2,4,1,0,3:T(8,128)S(1)} all-gather(f32[1,1,128,1,1,256]{5,2,4,1,0,3:T(8,128)S(1)} %copy.253), channel_id=11, replica_groups=mesh['batch'=1,'col'=4,'row'=8] {'col'}, dimensions={3}, use_global_device_ids=true | all-gather | bytes 655360 | tf_op jit(solution)/shard_map/all_gather | solution.py:27
  532.2 18.2 %all-gather.15.cloned.1.call-done = f32[1,8,128,256]{3,2,0,1:T(8,128)} async-done(((f32[1,1,128,256]{3,2,0,1:T(8,128)}), f32[1,8,128,256]{3,2,0,1:T(8,128)}) %all-gather.15.cloned.1.call-update) | async-done | bytes 1048592 | tf_op jit(solution)/shard_map/all_gather | solution.py:28
  551.6 2.5 convolution_bitcast_fusion
  554.2 11.3 %all-gather.8 = f32[1,1,128,1024]{3,2,1,0:T(8,128)S(1)} all-gather(f32[1,1,128,256]{3,2,1,0:T(8,128)S(1)} %get-tuple-element.39), channel_id=10, replica_groups=mesh['batch'=1,'col'=4,'row'=8] {'col'}, dimensions={3}, use_global_device_ids=true | all-gather | bytes 655360 | tf_op jit(solution)/shard_map/all_gather | solution.py:27
  565.8 9.0 %all-gather.19.cloned.1.call-done = f32[1024,256]{0,1:T(8,128)} async-done(((f32[128,256]{0,1:T(8,128)}), f32[1024,256]{0,1:T(8,128)}) %all-gather.19.cloned.1.call-update) | async-done | bytes 1048592 | tf_op jit(solution)/shard_map/all_gather | solution.py:28
  (88 shorter events, 30.7 us)
Async XLA Ops:
  6.5 113.2 %all-gather.17.cloned.1.call-start = ((), (), s32[]{:S(2)}) async-start(), calls=%async_computation.2 | async-start | bytes 10485760 | tf_op jit(solution)/shard_map/all_gather | solution.py:40
  29.5 3.0 copy-start
  386.2 15.5 %all-to-all-start = ((f32[8,1,2048]{2,1,0:T(1,128)}), f32[8,1,2048]{2,1,0:T(1,128)S(1)}, u32[]{:S(2)}, u32[]{:S(2)}) async-start(f32[8,1,2048]{2,1,0:T(1,128)} %reshape.229), calls=%async_computation | async-start | bytes 131072 | tf_op jit(solution)/shard_map/all_to_all | solution.py:51
  390.7 159.7 %all-gather.15.cloned.1.call-start = ((), (), s32[]{:S(2)}) async-start(), calls=%async_computation.1 | async-start | bytes 1179648 | tf_op jit(solution)/shard_map/all_gather | solution.py:28
  459.0 26.7 %copy-start.1 = (f32[2,64,16,4,8]{1,4,3,2,0:T(8,128)S(1)}, f32[2,64,16,4,8]{1,4,3,2,0:T(8,128)}, u32[]{:S(2)}) copy-start(f32[2,64,16,4,8]{1,4,3,2,0:T(8,128)} %copy.244) | copy-start | bytes 786436
  520.8 53.9 %all-gather.19.cloned.1.call-start = ((), (), s32[]{:S(2)}) async-start(), calls=%async_computation.3 | async-start | bytes 1179648 | tf_op jit(solution)/shard_map/all_gather | solution.py:28
Sparse Core Ops, SparseCore 0:
  32.5 87.2 all-gather.16
  520.9 29.3 all-gather.14
  554.3 20.4 all-gather.18
where the time goes:
time: 586 us; the launch traced here: 585 us
  blocking collectives  176 us (30%)
  other arithmetic  162 us (28%)
  local copies, waits for them, and re-layouts  116 us (20%)
  waiting for transfers between devices  101 us (17%)
  between operations  13.6 us (2%)
  matrix products  11.6 us (2%)
    another operation x5, other arithmetic, leaf_inverses(): lax.linalg.triangular_solve(natural, rhs_batch, left_side=True, lower=True)  160 us
    all_gather x4, blocking collectives, cyclic_product(): right_panel = natural_inner_rows(lax.all_gather(right, 'row', axis=1))  90.8 us
    all_gather x1, waiting for transfers between devices, leaf_inverses(): lax.all_gather(lax.all_gather(diag_blocks, 'row', axis=1), 'col', axis=3)  73.5 us
    reshape x2, local copies, waits for them, and re-layouts, leaf_inverses(): split_view.transpose(0, 2, 1, 3, 5, 4, 6)  66.2 us
    all_gather x6, blocking collectives, cyclic_product(): left_panel = natural_inner_cols(lax.all_gather(left, 'col', axis=2))  63.4 us
    all_gather x2, waiting for transfers between devices, cyclic_product(): right_panel = natural_inner_rows(lax.all_gather(right, 'row', axis=1))  27.1 us
    all_gather x1, blocking collectives, leaf_inverses(): lax.all_gather(diag_blocks, 'row', axis=1)  21.4 us
    reshape x1, local copies, waits for them, and re-layouts, leaf_inverses(): gathered.reshape(leaves, grid_rows, row_len // BLK, BLK, grid_cols, col_l...  21.1 us
  transfers between devices with their start and end apart: 4, of which 3 were waited for; matrix products, arithmetic and copies ran while one was open for 1% of the time, Pallas kernels for 0%

commit v1 on v0

v1 whole, which is shorter than its diff:
```python
import functools

import jax
import jax.numpy as jnp
from jax import lax
from jax.experimental import pallas as pl
from jax.experimental.pallas import tpu as pltpu
from jax.sharding import PartitionSpec as P

BLK = 8
CORES = 2
LANES = 128
MESH = pl.DeviceIdType.MESH
F32 = jnp.float32


def dot(left, right):
    return jnp.dot(left, right, precision=lax.Precision.HIGHEST, preferred_element_type=F32)


def iota(shape, dim):
    return lax.broadcasted_iota(jnp.int32, shape, dim)


def halves(tiles, half):
    low = iota(tiles[0].shape, 1) < LANES // 2
    out = []
    for first, second in ((tiles[0], tiles[1]), (tiles[2], tiles[3])):
        if half == 0:
            out.append(jnp.where(low, first, pltpu.roll(second, LANES // 2, 1)))
        else:
            out.append(jnp.where(low, pltpu.roll(first, LANES // 2, 1), second))
    return jnp.concatenate(out, axis=1)


class Net:
    def __init__(self, send, recv):
        self.send, self.recv, self.used, self.all = send, recv, 0, []

    def copy(self, src, dst, device):
        slot = self.used
        self.used += 1
        made = pltpu.make_async_remote_copy(
            src_ref=src, dst_ref=dst, send_sem=self.send.at[slot], recv_sem=self.recv.at[slot],
            device_id=device, device_id_type=MESH)
        return made

    def start(self, src, dst, device):
        made = self.copy(src, dst, device)
        made.start()
        self.all.append(made)
        return made


def kernel(rows, cols, l_ref, o_ref, U, G, C0, LF, PK, LI, W, ZM, ZS, TG, send, recv):
    chips = rows // CORES
    row = lax.axis_index("row")
    y = lax.axis_index("col")
    x, core = row // CORES, row % CORES
    spot, hh = row % cols, row // cols
    net = Net(send, recv)

    def at(xx, cc, yy):
        return {"row": xx * CORES + cc, "col": yy}

    def xs(step):
        return lax.rem(x + step + chips, chips)

    def ys(step):
        return lax.rem(y + step + cols, cols)

    partner = at(x, 1 - core, y)
    barrier = pltpu.get_barrier_semaphore()
    peers = [partner] + [at(xs(d), core, y) for d in range(1, chips)] + [at(x, core, ys(d)) for d in range(1, cols)]
    for peer in peers:
        pl.semaphore_signal(barrier, inc=1, device_id=peer, device_id_type=MESH)

    for part in range(2):
        piece = l_ref[part * 128:(part + 1) * 128, part * 256:(part + 1) * 256]
        low = iota((32, LANES), 1) < LANES // 2
        packed = [jnp.where(low, piece[64 * m:64 * m + 32, LANES * m:LANES * (m + 1)],
                            piece[64 * m + 32:64 * m + 64, LANES * m:LANES * (m + 1)]) for m in range(2)]
        packed.append(jnp.where(low, piece[32:64, :LANES], pltpu.roll(piece[96:128, LANES:], LANES // 2, 1)))
        packed += [piece[64:96, :LANES], piece[96:128, :LANES]]

        @pl.when(core == part)
        def _():
            for g in range(5):
                G[y, g, spot, :, hh] = packed[g].reshape(4, BLK, LANES)

        @pl.when(core != part)
        def _():
            for g in range(5):
                U[g] = packed[g].reshape(4, BLK, LANES)

    C0[y] = l_ref[128:256, 0:256]
    pl.semaphore_wait(barrier, len(peers))

    swap = net.start(U, G.at[y, :, spot, :, hh], partner)
    swap.wait_recv()

    def chip_piece(yy, g, xx, ysel=None):
        return G.at[yy if ysel is None else ysel, g, pl.ds(2 * (xx % 2), 2), :, xx // 2]

    axis_first = ["x", "y", "y", "x", "y"]
    first = []
    for g in range(5):
        mine = chip_piece(y, g, x)
        if axis_first[g] == "x":
            first.append([net.start(mine, mine, at(xs(d), core, y)) for d in range(1, chips)])
        else:
            first.append([net.start(mine, mine, at(x, core, ys(d))) for d in range(1, cols)])
    c0_src = l_ref.at[pl.ds(128, 128), pl.ds(0, 256)]

    def bundle(g, step, part=None):
        if axis_first[g] == "x":
            return G.at[ys(step), g] if part is None else G.at[ys(step), g, pl.ds(2 * part, 2)]
        sel = slice(None) if part is None else pl.ds(2 * part, 2)
        return chip_piece(None, g, xs(step), sel)

    def along(g, step):
        return at(x, core, ys(step)) if axis_first[g] == "x" else at(xs(step), core, y)

    second = {}

    def send_second(g):
        for made in first[g]:
            made.wait_recv()
        second[g] = [net.start(bundle(g, 0), bundle(g, 0), along(g, 1)),
                     net.start(bundle(g, 0), bundle(g, 0), along(g, -1))]

    def relay(g):
        up, down = second[g]
        up.wait_recv()
        far_up = net.start(bundle(g, -1, 0), bundle(g, -1, 0), along(g, 1))
        down.wait_recv()
        far_down = net.start(bundle(g, 1, 1), bundle(g, 1, 1), along(g, -1))
        second[g] = [far_up, far_down]

    def arrive(g):
        for made in second[g]:
            made.wait_recv()

    for g in range(5):
        send_second(g)
    c0_copies = [net.start(c0_src, C0.at[y], at(x, core, ys(d))) for d in range(1, cols)]
    for g in range(2):
        relay(g)
    for g in range(2):
        arrive(g)

    lane = iota((BLK, LANES), 1)
    sub = iota((BLK, LANES), 0)
    block_of = (lane // BLK) % BLK
    diag = [[[None] * 4 for _ in range(4)] for _ in range(2)]
    inv = [[[None] * 4 for _ in range(4)] for _ in range(2)]
    for m in range(2):
        for c in range(4):
            for k in range(c + 1):
                total = jnp.zeros((BLK, LANES), F32)
                for b in range(8):
                    total = jnp.where(block_of == b, G[k, m, c, b // 2, b % 2], total)
                diag[m][c][k] = total
                inv[m][c][k] = jnp.where(sub == lane % BLK, 1.0, 0.0) if c == k else jnp.zeros((BLK, LANES), F32)
    for t in range(32):
        ct, jt = t // BLK, t % BLK
        index = (lane // BLK) * BLK + jt
        for m in range(2):
            spread = [jnp.take_along_axis(diag[m][c][ct], index, axis=1) for c in range(ct, 4)]
            pivot = 1.0 / spread[0][jt:jt + 1, :]
            below = jnp.where(sub > jt, spread[0], 0.0)
            for k in range(ct + 1):
                solved = inv[m][ct][k][jt:jt + 1, :] * pivot
                inv[m][ct][k] = jnp.where(sub == jt, solved, inv[m][ct][k] - below * solved)
                for c in range(ct + 1, 4):
                    inv[m][c][k] = inv[m][c][k] - spread[c - ct] * solved
    for m in range(2):
        for c in range(4):
            tiles = [inv[m][c][k] if k <= c else jnp.zeros((BLK, LANES), F32) for k in range(4)]
            for e in range(2):
                PK[2 * m + e, c] = halves(tiles, e)
    wide_block = (iota((BLK, 2 * LANES), 1) % 64) // BLK

    @pl.loop(0, 2)
    def _(m):
        tiles = [G[k, m].reshape(256, LANES) for k in range(4)]
        for e in range(2):
            LF[2 * m + e] = halves(tiles, e).reshape(32, BLK, 256)

    def keep(mask, tile):
        return jnp.where(mask, tile, 0.0)

    def double(leaf, nb):
        group = wide_block // nb
        packed = [PK[leaf, i] for i in range(4 * nb)]
        spread = jnp.concatenate([keep(group == b // nb, packed[(b % nb) * 4 + c]) for c in range(4) for b in range(8)], axis=0)
        coupling = []
        for bb in range(nb):
            for c in range(4):
                total = None
                for s in range(1, 8 // nb, 2):
                    tile = LF[leaf, c * 8 + s * nb + bb]
                    total = keep(group == s - 1, tile if total is None else tile) if total is None else jnp.where(group == s - 1, tile, total)
                coupling.append(total)
        temp = dot(jnp.concatenate(coupling, axis=0), spread)
        zero = jnp.zeros((BLK, 256), F32)
        temp_spread = jnp.concatenate(
            [keep(group == b // nb - 1, temp[((b % nb) * 4 + c) * BLK:((b % nb) * 4 + c + 1) * BLK]) if (b // nb) % 2 else zero
             for c in range(4) for b in range(8)], axis=0)
        corner = dot(jnp.concatenate(packed, axis=0), temp_spread)
        for half in range(2):
            for i in range(4 * nb):
                tile = keep(group % 2 == half, packed[i])
                if half:
                    tile = tile - corner[i * BLK:(i + 1) * BLK]
                if nb < 4:
                    PK[leaf, half * 4 * nb + i] = tile
                else:
                    bb, c = i // 4, i % 4
                    LI[leaf, c * 8 + half * 4 + bb] = tile

    for step, nb in enumerate((1, 2, 4)):
        @pl.loop(0, 2)
        def _(m):
            for e in range(2):
                double(2 * m + e, nb)
        relay(2 + step)

    def leaf_inv(i):
        return LI[i].reshape(256, 256)

    for g in range(2, 5):
        arrive(g)

    def coupling2(m):
        return halves([G[k, 2].reshape(256, LANES) for k in range(4)], m)

    def coupling1(g):
        return jnp.concatenate([G[k, g].reshape(256, LANES) for k in range(4)], axis=1)

    def pick(i):
        r, l = iota((256, 256), 0), iota((256, 256), 1)
        return jnp.where((r // 64 == y) & (l // 64 == i) & (r % 64 == l % 64), 1.0, 0.0)

    send_w = net.copy(W, W, partner)
    send_z = net.copy(ZS, ZM, partner)

    @pl.when(core == 0)
    def _():
        def put(i, val):
            W[i // 2, :, i % 2] = val.reshape(4, 4, 2, BLK, 256)
            return val

        w0 = put(0, dot(leaf_inv(0), pick(0)))
        w1 = put(1, dot(leaf_inv(1), pick(1) - dot(coupling2(0), w0)))
        pair = W[0].reshape(512, 256)
        s2 = pick(2) - dot(coupling1(3), pair)
        s3 = pick(3) - dot(coupling1(4), pair)
        w2 = put(2, dot(leaf_inv(2), s2))
        put(3, dot(leaf_inv(3), s3 - dot(coupling2(1), w2)))
        send_w.start()

    @pl.when(core == 1)
    def _():
        def mine(i):
            r, l = iota((256, 256), 0), iota((256, 256), 1)
            own = CORES * x + r // 128
            return jnp.where(((r // 32) % 4 == i) & (l // 64 == own % cols) & ((l % 64) // BLK == 2 * ((r // BLK) % 4) + own // cols)
                             & (r % BLK == l % BLK), 1.0, 0.0)

        def put(i, val):
            ZS[i] = val[:128]
            ZM[i] = val[128:]
            return val

        z3 = put(3, dot(mine(3), leaf_inv(3)))
        z2 = put(2, dot(mine(2) - dot(z3, coupling2(1)), leaf_inv(2)))
        both = dot(z2, coupling1(3)) + dot(z3, coupling1(4))
        tiles = [both[:, LANES * k:LANES * (k + 1)] for k in range(4)]
        z1 = put(1, dot(mine(1) - halves(tiles, 1), leaf_inv(1)))
        put(0, dot(mine(0) - halves(tiles, 0) - dot(z1, coupling2(0)), leaf_inv(0)))
        send_z.start()

    for made in c0_copies:
        made.wait_recv()

    @pl.when(core == 0)
    def _():
        send_z.wait_recv()

    @pl.when(core == 1)
    def _():
        send_w.wait_recv()

    left = jnp.concatenate([C0[k, :, LANES * n:LANES * (n + 1)] for n in range(2) for k in range(4)], axis=1)
    TG[:, spot, :, hh] = dot(left, W[...].reshape(1024, 256)).reshape(4, 4, BLK, 256)

    def t_piece(xx, cc):
        own = CORES * xx + cc
        return TG.at[:, own % cols, :, own // cols]

    t_out = [net.start(t_piece(x, core), t_piece(x, core), at(xs(d), core, y)) for d in range(1, chips)]
    t_in = [net.start(t_piece(x, core), t_piece(x, core), partner)]

    o_ref[0:128, 256:512] = jnp.zeros((128, 256), F32)
    for i in range(4):
        o_ref[32 * i:32 * (i + 1), 0:256] = W[i // 2, spot, i % 2, :, hh].reshape(32, 256)
    o_ref[128:256, 256:512] = sum(dot(ZM[i], pick(i)) for i in range(4))

    for d, made in enumerate(t_out):
        made.wait_recv()
        there = t_piece(xs(-(d + 1)), core)
        t_in.append(net.start(there, there, partner))
    for made in t_in:
        made.wait_recv()
    o_ref[128:256, 0:256] = -sum(dot(ZM[i], TG[i].reshape(256, 256)) for i in range(4))

    for made in net.all:
        made.wait_send()

    @pl.when(core == 0)
    def _():
        send_w.wait_send()

    @pl.when(core == 1)
    def _():
        send_z.wait_send()


def solution(mesh):
    rows, cols = mesh.shape["row"], mesh.shape["col"]
    block_spec = P(("batch", "row"), "col")

    def device_body(local_l):
        vmem = functools.partial(pltpu.VMEM, dtype=F32)
        slots = 64
        return pl.pallas_call(
            functools.partial(kernel, rows, cols),
            out_shape=jax.ShapeDtypeStruct(local_l.shape, F32),
            in_specs=[pl.BlockSpec(memory_space=pltpu.VMEM)],
            out_specs=pl.BlockSpec(memory_space=pltpu.VMEM),
            scratch_shapes=[
                vmem((5, 4, BLK, LANES)),
                vmem((4, 5, 4, 4, 2, BLK, LANES)),
                vmem((4, 128, 256)),
                vmem((4, 32, BLK, 256)),
                vmem((4, 16, BLK, 256)),
                vmem((4, 32, BLK, 256)),
                vmem((2, 4, 2, 4, 2, BLK, 256)),
                vmem((4, 128, 256)),
                vmem((4, 128, 256)),
                vmem((4, 4, 4, 2, BLK, 256)),
                pltpu.SemaphoreType.DMA((slots,)),
                pltpu.SemaphoreType.DMA((slots,)),
            ],
            compiler_params=pltpu.CompilerParams(collective_id=0, has_side_effects=True),
        )(local_l)

    return jax.shard_map(device_body, mesh=mesh, in_specs=(block_spec,), out_specs=block_spec, check_vma=False)
```

time: 586 us -> 58.7 us (0.10)
  blocking collectives: 176 us -> 0 us
  other arithmetic: 162 us -> 0 us
  local copies, waits for them, and re-layouts: 116 us -> 1.87 us
  waiting for transfers between devices: 101 us -> 0 us
  Pallas kernels: 0 us -> 56.7 us
  between operations: 13.6 us -> 0.01 us
  matrix products: 11.6 us -> 0 us
    all_gather x11 -> x0, blocking collectives: 176 us -> none  [the longest x4 90.8 us: cyclic_product(): right_panel = natural_inner_rows(lax.all_gather(right, 'row', axis=1))]
    another operation x7 -> x0, other arithmetic: 160 us -> none  [the longest x5 160 us: leaf_inverses(): lax.linalg.triangular_solve(natural, rhs_batch, left_side=True, lower=True)]
    all_gather x3 -> x0, waiting for transfers between devices: 101 us -> none  [the longest x1 73.5 us: leaf_inverses(): lax.all_gather(lax.all_gather(diag_blocks, 'row', axis=1), 'col', axis=3)]
    reshape x12 -> x0, local copies, waits for them, and re-layouts: 91.3 us -> none  [the longest x2 66.2 us: leaf_inverses(): split_view.transpose(0, 2, 1, 3, 5, 4, 6)]
    pallas_call x0 -> x1, Pallas kernels: none -> 56.7 us  [device_body(): pl.pallas_call(functools.partial(kernel, rows, cols), out_shape=jax.Shape...]
    all_gather x9 -> x0, local copies, waits for them, and re-layouts: 11.6 us -> none  [the longest x1 6.26 us: leaf_inverses(): lax.all_gather(lax.all_gather(diag_blocks, 'row', axis=1), 'col', axis=3)]
    dot_general x6 -> x0, matrix products: 7.51 us -> none  [highest_matmul(): jnp.einsum('sik,skj->sij', left, right, precision=lax.Precision.HIGHEST,...]
    another operation x11 -> x0, local copies, waits for them, and re-layouts: 6.34 us -> none
  transfers between devices with their start and end apart: 4 -> 0, of which waited for: 3 -> 0; matrix products, arithmetic and copies ran while one was open for 1% -> 0% of each run, Pallas kernels for 0% -> 0%
where the time goes in v1:
time: 58.7 us; the launch traced here: 58.5 us
  Pallas kernels  56.7 us (97%)
  local copies, waits for them, and re-layouts  1.87 us (3%)
    pallas_call x1, Pallas kernels, device_body(): pl.pallas_call(functools.partial(kernel, rows, cols), out_shape=jax.Shape...  56.7 us
    unnamed x1, local copies, waits for them, and re-layouts  1.87 us

profile of v1, /device:TPU:97, one launch (start us, length us, event | category | flops | bytes accessed | tf_op | source)
XLA Modules:
  0.0 58.5 jit_solution(17689883772286909896)
XLA Ops:
  0.0 56.7 %shard_map.17 = f32[256,512]{1,0:T(8,128)} custom-call(f32[256,512]{1,0:T(8,128)} %l_ref.1), custom_call_target="tpu_custom_call" | custom-call | tf_op jit(solution)/shard_map/pallas_call | solution.py:337
  56.7 1.9 %copy.3 = f32[256,512]{1,0:T(8,128)} copy(f32[256,512]{1,0:T(8,128)} %shard_map.17) | data formatting | bytes 1048576
